TPU v7x, 32 devices: a whole 2x2x4 slice. The times are simulated.
32 devices in a mesh: dp: 8 (over z, x), mp: 4 (over y, core).
Axes of the slice: x: 2, y: 2, z: 4, core: 2. Of those that a mesh axis runs over, the one named last changes fastest.
Arguments:
- vision_rows: bfloat16 [1024, 1024], P('dp'), may hold values from -6 to 6
- image_count: int32 [32], P('dp'), may hold values from 0 to 4
- proj_flat: bfloat16 [32768, 128], P(('dp', 'mp')), may hold values from -0.1875 to 0.1875
- text_embeds: bfloat16 [3072, 4096], P(('dp', 'mp')), may hold values from -6 to 6
- norm_gain: float32 [4096], replicated, may hold values from 0.1 to 1.9
- q_weight: bfloat16 [4096, 4096], P(None, 'mp'), may hold values from -0.09375 to 0.09375
- q_grad: bfloat16 [4096, 4096], P('dp', 'mp'), may hold values from -6 to 6
Outputs:
- text_grad: bfloat16 [3072, 4096], P(('dp', 'mp'))
- proj_grad: float32 [32768, 128], P(('dp', 'mp'))
Inputs may be any that keep to these rules, and one draw needn't show every extreme that they name: Slot s of device k holds an image when s < image_count[k]; other slots are padding.
All inputs are finite; a program needn't handle non-finite values.
Results may differ from a plain program's by a relative error of at most 0.014.
Values may be sent and summed in bfloat16 or wider, within the bound.
A program may use at most 64 MiB of HBM per device.

v0:
```python
import jax
import jax.numpy as jnp
from jax import lax
from jax.sharding import PartitionSpec as P

IMG_MAX = 4
PATCH = 8
ROWS_DEV = 128


norm_eps = 1e-05


def row_term(left, weight):
    return lax.dot_general(
        left, weight, (((1,), (1,)), ((), ())), preferred_element_type=jnp.float32
    )


def norm_back(rows_in, grads, gain):
    inputs = rows_in.astype(jnp.float32)
    inv_rms = lax.rsqrt(jnp.mean(inputs * inputs, axis=-1, keepdims=True) + norm_eps)
    scaled = gain[None, :] * grads
    inner_mean = jnp.mean(scaled * inputs, axis=-1, keepdims=True)
    return inv_rms * scaled - inputs * inv_rms**3 * inner_mean


def body(vision_rows, image_count, proj_flat, text_embeds, norm_gain, q_weight, q_grad):
    groups = lax.axis_size("mp")
    member = lax.axis_index("mp")
    shards = lax.axis_size("dp")
    enc_width = vision_rows.shape[1]
    block_cols = q_weight.shape[1]
    model_width = q_weight.shape[0]
    used_count = enc_width * block_cols
    image_rows = IMG_MAX * PATCH
    gathered = lax.all_gather(proj_flat, "dp", axis=0, tiled=True)
    proj_block = gathered.reshape(-1)[:used_count].reshape(enc_width, block_cols)
    embed_cols = jnp.dot(vision_rows, proj_block, preferred_element_type=jnp.float32).astype(
        jnp.bfloat16
    )
    row_ids = jnp.arange(groups * image_rows, dtype=jnp.int32)
    owners = row_ids // image_rows
    slot_ids = row_ids % image_rows // PATCH
    owner_match = owners[:, None] == jnp.arange(groups, dtype=jnp.int32)[None, :]
    owner_counts = jnp.sum(jnp.where(owner_match, image_count[None, :], 0), axis=1)
    live_group = (slot_ids < owner_counts)[:, None]
    blocks = q_grad.reshape(groups, ROWS_DEV, block_cols)
    image_query = blocks[:, :image_rows].reshape(-1, block_cols)
    text_query = blocks[:, image_rows:].reshape(-1, block_cols)
    image_term = row_term(image_query, q_weight)
    image_norm = lax.psum_scatter(
        image_term.astype(jnp.bfloat16), "mp", scatter_dimension=1, tiled=True
    ).astype(jnp.float32)
    text_norm = lax.psum_scatter(
        row_term(text_query, q_weight).astype(jnp.bfloat16), "mp", scatter_dimension=0, tiled=True
    ).astype(jnp.float32)
    x_cols = embed_cols.astype(jnp.float32)
    gain_cols = lax.dynamic_slice_in_dim(norm_gain, member * block_cols, block_cols)
    scaled = gain_cols[None, :] * image_norm
    squares, inner_sum = lax.psum(
        (jnp.sum(x_cols * x_cols, axis=1), jnp.sum(scaled * x_cols, axis=1)), "mp"
    )
    inv_rms = lax.rsqrt(squares / model_width + norm_eps)[:, None]
    image_input = inv_rms * scaled - x_cols * inv_rms**3 * (inner_sum / model_width)[:, None]
    image_cols = jnp.where(live_group, image_input, 0.0).astype(jnp.bfloat16)
    text_grad = norm_back(text_embeds, text_norm, norm_gain).astype(jnp.bfloat16)
    grad_scale = 1.0 / jnp.sqrt(jnp.float32(shards * groups * image_rows))
    proj_part = (
        lax.dot_general(
            vision_rows, image_cols, (((0,), (0,)), ((), ())), preferred_element_type=jnp.float32
        )
        * grad_scale
    )
    stored_rows = proj_flat.shape[0]
    padded = jnp.pad(proj_part.reshape(-1), (0, shards * stored_rows * 128 - used_count))
    padded = padded.reshape(shards * stored_rows, 128)
    proj_grad = lax.psum_scatter(padded, "dp", scatter_dimension=0, tiled=True)
    return (text_grad, proj_grad)


def solution(mesh):
    return jax.shard_map(
        body,
        mesh=mesh,
        in_specs=(
            P("dp", None),
            P("dp"),
            P(("dp", "mp"), None),
            P(("dp", "mp"), None),
            P(),
            P(None, "mp"),
            P("dp", "mp"),
        ),
        out_specs=(P(("dp", "mp"), None), P(("dp", "mp"), None)),
        check_vma=False,
    )
```

profile of v0, /device:TPU:0, one launch (start us, length us, event | category | flops | bytes accessed | tf_op | source)
XLA Modules:
  0.0 185.0 jit_solution(15927528235319650530)
XLA Ops:
  8.0 0.0 copy-start
  8.0 0.0 all-gather.2.cloned.1.call-start
  8.1 0.7 all-gather.2.cloned.1.call-update
  8.7 0.0 reduce-scatter.6.cloned.1.call-start
  8.8 1.0 slice.9
  9.8 0.0 copy-start.4
  9.8 7.3 %convolution_convert_fusion.1 = bf16[128,4096]{1,0:T(8,128)(2,1)} fusion(bf16[128,1024]{1,0:T(8,128)(2,1)S(1)} %bitcast.12, bf16[4096,1024]{1,0:T(8,128)(2,1)} %param.12), kind=kOutput, calls=%fused_computation.1 | convolution fusion | flops 1074266112 | bytes 9699328 | tf_op jit(solution)/shard_map/dot_general | solution.py:15
  17.1 0.0 reduce-scatter.6.cloned.1.call-update
  17.1 0.0 reduce-scatter.4.cloned.1.call-start
  17.2 0.0 copy-done.4
  17.2 0.1 slice.8
  17.3 10.3 %convolution_convert_fusion = bf16[384,4096]{1,0:T(8,128)(2,1)} fusion(bf16[384,1024]{1,0:T(8,128)(2,1)S(1)} %bitcast.15, bf16[4096,1024]{1,0:T(8,128)(2,1)} %param.12), kind=kOutput, calls=%fused_computation | convolution fusion | flops 3222798336 | bytes 12320768 | tf_op jit(solution)/shard_map/dot_general | solution.py:15
  27.6 0.0 reduce-scatter.4.cloned.1.call-update
  27.6 0.0 reduce-scatter.8.cloned.1.call-start
  27.7 0.6 copy-done.5
  28.3 0.1 select_reduce_fusion
  28.4 34.4 %all-gather.2.cloned.1.call-done = bf16[8192,128]{1,0:T(8,128)(2,1)} async-done(((bf16[1024,128]{1,0:T(8,128)(2,1)}), bf16[8192,128]{1,0:T(8,128)(2,1)}) %all-gather.2.cloned.1.call-update) | async-done | bytes 2097168 | tf_op jit(solution)/shard_map/all_gather | solution.py:37
  62.8 3.0 %reshape_reshape.3 = bf16[1024,1024]{1,0:T(8,128)(2,1)S(1)} reshape(bf16[8192,128]{1,0:T(8,128)(2,1)} %all-gather.2.cloned.1.call-done) | data formatting | bytes 4194304 | tf_op jit(solution)/shard_map/reshape;reshape | solution.py:38
  65.8 0.0 reduce-scatter.6.cloned.1.call-done
  65.9 0.0 copy-done
  65.9 0.0 copy-start.3
  65.9 1.6 multiply_reduce_fusion.1
  67.5 6.5 %all-reduce = (f32[128]{0:T(128)S(1)}, f32[128]{0:T(128)S(1)}) all-reduce(f32[128]{0:T(128)S(1)} %get-tuple-element.5, f32[128]{0:T(128)S(1)} %get-tuple-element.4), channel_id=1, replica_groups=mesh['dp'=8,'mp'=4] {'mp'}, use_global_device_ids=true, to_apply=%region_8.9 | all-reduce | flops 256 | bytes 2048 | tf_op jit(solution)/shard_map/psum | solution.py:61
  73.9 2.8 %multiply_bitcast_fusion = f32[1024,1024]{0,1:T(8,128)} fusion(bf16[128,1024]{1,0:T(8,128)(2,1)S(1)} %copy-done, f32[128,1024]{1,0:T(8,128)S(1)} %get-tuple-element.12, bf16[128,1024]{1,0:T(8,128)(2,1)S(1)} %copy-done.3, f32[128]{0:T(128)S(1)} %get-tuple-element.13, f32[128]{0:T(128)S(1)} %get-tuple-element.9, f32[1024]{0:T(1024)S(1)} %dynamic_slice.3, ...), kind=kOutput, calls=%fused_computation.2 | convolution fusion | flops 270532608 | bytes 5248640 | tf_op jit(solution)/shard_map/dot_general | solution.py:70
  76.7 5.4 %copy.10 = f32[1024,1024]{1,0:T(8,128)} copy(f32[1024,1024]{0,1:T(8,128)} %multiply_bitcast_fusion) | data formatting | bytes 8388608 | tf_op jit(solution)/shard_map/mul | solution.py:70
  82.1 4.9 %reshape.87 = f32[8192,128]{1,0:T(8,128)} reshape(f32[1024,1024]{1,0:T(8,128)} %copy.10) | data formatting | bytes 8388608 | tf_op jit(solution)/shard_map/reshape | solution.py:77
  87.0 0.0 reduce-scatter.8.cloned.1.call-update
  87.0 0.0 reduce-scatter.4.cloned.1.call-done
  87.1 1.1 copy-done.1
  88.1 1.7 fusion
  89.8 1.3 fusion.3
  91.2 86.2 %reduce-scatter.8.cloned.1.call-done = f32[1024,128]{1,0:T(8,128)} async-done(((f32[8192,128]{1,0:T(8,128)}), f32[1024,128]{1,0:T(8,128)}) %reduce-scatter.8.cloned.1.call-update) | async-done | bytes 524304 | tf_op jit(solution)/shard_map/reduce_scatter | solution.py:78
  (13 shorter events, 0.1 us)
Async XLA Ops:
  8.0 57.9 %copy-start = (bf16[128,1024]{1,0:T(8,128)(2,1)S(1)}, bf16[128,1024]{1,0:T(8,128)(2,1)}, u32[]{:S(2)}) copy-start(bf16[128,1024]{1,0:T(8,128)(2,1)} %param.7) | copy-start | bytes 786436
  8.0 54.8 %all-gather.2.cloned.1.call-start = ((), (), s32[]{:S(2)}) async-start(), calls=%async_computation.4 | async-start | bytes 2359296 | tf_op jit(solution)/shard_map/all_gather | solution.py:37
  8.7 57.1 %reduce-scatter.6.cloned.1.call-start = ((), (), s32[]{:S(2)}) async-start(), calls=%async_computation.5 | async-start | bytes 1310720 | tf_op jit(solution)/shard_map/reduce_scatter | solution.py:52
  9.8 7.4 %copy-start.4 = (bf16[512,1024]{1,0:T(8,128)(2,1)S(1)}, bf16[512,1024]{1,0:T(8,128)(2,1)}, u32[]{:S(2)}) copy-start(bf16[512,1024]{1,0:T(8,128)(2,1)} %param.13) | copy-start | bytes 3145732
  17.1 69.9 %reduce-scatter.4.cloned.1.call-start = ((), (), s32[]{:S(2)}) async-start(), calls=%async_computation.3 | async-start | bytes 3932160 | tf_op jit(solution)/shard_map/reduce_scatter | solution.py:55
  27.6 0.7 copy-start.5
  27.6 0.7 copy-start.6
  27.6 149.7 %reduce-scatter.8.cloned.1.call-start = ((), (), s32[]{:S(2)}) async-start(), calls=%async_computation.6 | async-start | bytes 4718592 | tf_op jit(solution)/shard_map/reduce_scatter | solution.py:78
  65.9 8.1 %copy-start.3 = (bf16[128,1024]{1,0:T(8,128)(2,1)S(1)}, bf16[128,1024]{1,0:T(8,128)(2,1)}, u32[]{:S(2)}) copy-start(bf16[128,1024]{1,0:T(8,128)(2,1)} %reduce-scatter.6.cloned.1.call-done) | copy-start | bytes 786436
  87.0 1.1 copy-start.1
  88.1 1.7 copy-start.2
Sparse Core Ops, SparseCore 0:
  10.9 51.8 all-gather.1
Sparse Core Ops, SparseCore 1:
  17.2 27.4 reduce-scatter.5
  47.1 37.8 reduce-scatter.3
  89.1 88.2 reduce-scatter.7
where the time goes:
time: 185 us
  waiting for transfers between devices  121 us (65%)
  matrix products  22.1 us (12%)
  local copies, waits for them, and re-layouts  16 us (9%)
  between operations  15.8 us (9%)
  blocking collectives  6.48 us (4%)
  other arithmetic  3.11 us (2%)
    reduce_scatter x1, waiting for transfers between devices, body(): proj_grad = lax.psum_scatter(padded, 'dp', scatter_dimension=0, tiled=True)  86.2 us
    all_gather x1, waiting for transfers between devices, body(): gathered = lax.all_gather(proj_flat, 'dp', axis=0, tiled=True)  34.4 us
    dot_general x2, matrix products, row_term(): lax.dot_general(left, weight, (((1,), (1,)), ((), ())), preferred_element...  17.7 us
    psum x1, blocking collectives, body(): lax.psum((jnp.sum(x_cols * x_cols, axis=1), jnp.sum(scaled * x_cols, axis...  6.48 us
    mul x1, local copies, waits for them, and re-layouts, body(): lax.dot_general(vision_rows, image_cols, (((0,), (0,)), ((), ())), prefer...  5.36 us
    reshape x1, local copies, waits for them, and re-layouts, body(): padded = padded.reshape(shards * stored_rows, 128)  4.91 us
  transfers between devices with their start and end apart: 4, of which 2 were waited for; matrix products, arithmetic and copies ran while one was open for 21% of the time, Pallas kernels for 0%

commit v1 on v0

--- a/solution.py
+++ b/solution.py
@@ -1,12 +1,22 @@
+import functools
+
 import jax
 import jax.numpy as jnp
 from jax import lax
+from jax.experimental import pallas as pl
+from jax.experimental.pallas import tpu as pltpu
 from jax.sharding import PartitionSpec as P
 
 IMG_MAX = 4
 PATCH = 8
 ROWS_DEV = 128
-
+CORES = 2
+SIDE = 2
+CHUNKS = 2
+TILE = 256
+ROW_STEP = 16
+
+MESH = pl.DeviceIdType.MESH
 
 norm_eps = 1e-05
 
@@ -15,6 +25,479 @@
     return lax.dot_general(
         left, weight, (((1,), (1,)), ((), ())), preferred_element_type=jnp.float32
     )
+
+
+class LineGather:
+    def __init__(self, depth, me, member, own, buf, send, recv):
+        self.depth, self.me, self.member = depth, me, member
+        self.z, self.x = me // SIDE, me % SIDE
+        self.own, self.buf, self.send, self.recv = own, buf, send, recv
+        self.step = buf.shape[1] // CHUNKS
+
+    def rows(self, chunk):
+        return pl.ds(chunk * self.step, self.step)
+
+    def copy(self, zz, x, chunk, way, own=False):
+        block = zz * SIDE + x
+        place = self.buf.at[block, self.rows(chunk)]
+        target = (self.me + SIDE, self.me - SIDE, self.z * SIDE + (1 - self.x))[way]
+        return pltpu.make_async_remote_copy(
+            src_ref=self.own.at[self.rows(chunk)] if own else place,
+            dst_ref=place,
+            send_sem=self.send.at[way, zz, chunk],
+            recv_sem=self.recv.at[block, chunk],
+            device_id=(target, self.member),
+            device_id_type=MESH,
+        )
+
+    def start(self):
+        for chunk in range(CHUNKS):
+            @pl.when(self.z < self.depth - 1)
+            def _():
+                self.copy(self.z, self.x, chunk, 0, True).start()
+
+            @pl.when(self.z > 0)
+            def _():
+                self.copy(self.z, self.x, chunk, 1, True).start()
+
+            self.copy(self.z, self.x, chunk, 2, True).start()
+
+    def relay(self, hop, chunk):
+        below, above = self.z - hop, self.z + hop
+
+        @pl.when(below >= 0)
+        def _():
+            self.copy(below, self.x, chunk, 0).wait_recv()
+
+            @pl.when(self.z < self.depth - 1)
+            def _():
+                self.copy(below, self.x, chunk, 0).start()
+
+            self.copy(below, self.x, chunk, 2).start()
+
+        @pl.when(above < self.depth)
+        def _():
+            self.copy(above, self.x, chunk, 1).wait_recv()
+
+            @pl.when(self.z > 0)
+            def _():
+                self.copy(above, self.x, chunk, 1).start()
+
+            self.copy(above, self.x, chunk, 2).start()
+
+    def line_blocks(self, hop, use):
+        for zz in (self.z - hop, self.z + hop):
+            @pl.when((zz >= 0) & (zz < self.depth))
+            def _():
+                use(zz * SIDE + self.x)
+
+    def side_blocks(self, hop, use):
+        for zz in (self.z,) if hop == 0 else (self.z - hop, self.z + hop):
+            @pl.when((zz >= 0) & (zz < self.depth))
+            def _():
+                for chunk in range(CHUNKS):
+                    self.copy(zz, 1 - self.x, chunk, 2).wait_recv()
+                use(zz * SIDE + 1 - self.x)
+
+    def drain(self):
+        for zz in range(self.depth):
+            for chunk in range(CHUNKS):
+                @pl.when((self.z >= zz) & (self.z < self.depth - 1))
+                def _():
+                    self.copy(zz, self.x, chunk, 0).wait_send()
+
+                @pl.when((self.z <= zz) & (self.z > 0))
+                def _():
+                    self.copy(zz, self.x, chunk, 1).wait_send()
+
+                self.copy(zz, self.x, chunk, 2).wait_send()
+
+
+def kernel(
+    shards, groups, grad_scale,
+    proj_ref, vision_ref, live_ref, gain_ref, q_hbm, w_hbm, text_hbm,
+    text_out, proj_out,
+    qv, wv, tv, own_text, own_image, mate_text, mate_image, sum_text, sum_image,
+    far_text, far_image, scaled_image, x_acc, g_acc, g_own, stat_own, stats,
+    w_all, g_all, v_all,
+    q_sem, w_sem, t_sem, a_send, a_recv, c_send, c_recv, v_send, v_recv,
+    mt_send, mt_recv, mi_send, mi_recv, ft_send, ft_recv, fi_send, fi_recv, s_send, s_recv,
+):
+    me, member = lax.axis_index("dp"), lax.axis_index("mp")
+    depth = shards // SIDE
+    chips = groups // CORES
+    y, core = member // CORES, member % CORES
+    mate = y * CORES + 1 - core
+    shard_k, block_cols = proj_ref.shape
+    image_rows = vision_ref.shape[0]
+    per_image = image_rows // groups
+    rows_dev = qv.shape[0] // groups
+    text_rows = rows_dev - per_image
+    width = groups * block_cols
+    f32, bf16 = jnp.float32, jnp.bfloat16
+
+    far = [lax.rem(y + step, chips) for step in range(1, chips)]
+    order = [yy * CORES + lax.rem(core + flip, CORES) for yy in far + [y] for flip in (1, 0)]
+    early = len(order) // 2
+
+    q_copy = pltpu.make_async_copy(q_hbm, qv, q_sem)
+    q_copy.start()
+    w_copies = [pltpu.make_async_copy(w_hbm.at[j], wv.at[j], w_sem.at[k]) for k, j in enumerate(order)]
+    for copy in w_copies:
+        copy.start()
+    t_copy = pltpu.make_async_copy(text_hbm, tv, t_sem)
+    t_copy.start()
+
+    barrier = pltpu.get_barrier_semaphore()
+    for step in range(1, shards):
+        pl.semaphore_signal(
+            barrier, inc=1, device_id=(lax.rem(me + step, shards), member), device_id_type=MESH
+        )
+    for step in range(1, groups):
+        pl.semaphore_signal(
+            barrier, inc=1, device_id=(me, lax.rem(member + step, groups)), device_id_type=MESH
+        )
+    pl.semaphore_wait(barrier, shards + groups - 2)
+
+    weights = LineGather(depth, me, member, proj_ref, w_all, a_send, a_recv)
+    weights.start()
+
+    def remote(src, dst, send, recv, device):
+        return pltpu.make_async_remote_copy(
+            src_ref=src, dst_ref=dst, send_sem=send, recv_sem=recv,
+            device_id=device, device_id_type=MESH,
+        )
+
+    def text_to_mate(k):
+        j = order[k]
+        return remote(own_text.at[j, 1 - core], mate_text.at[j], mt_send.at[j], mt_recv.at[j], (me, mate))
+
+    def image_to_mate(yy):
+        return remote(
+            own_image.at[yy * CORES + 1 - core], mate_image.at[yy],
+            mi_send.at[yy], mi_recv.at[yy], (me, mate),
+        )
+
+    def text_to_far(k, yy):
+        j = order[k]
+        return remote(
+            sum_text.at[j, yy], far_text.at[y, j], ft_send.at[j, yy], ft_recv.at[y, j],
+            (me, yy * CORES + core),
+        )
+
+    def text_from_far(k, yy):
+        j = order[k]
+        return remote(
+            sum_text.at[j, yy], far_text.at[yy, j], ft_send.at[j, yy], ft_recv.at[yy, j],
+            (me, yy * CORES + core),
+        )
+
+    def image_to_far(yy):
+        return remote(
+            sum_image.at[yy], far_image.at[y], fi_send.at[yy], fi_recv.at[y], (me, yy * CORES + core)
+        )
+
+    def image_from_far(yy):
+        return remote(
+            sum_image.at[yy], far_image.at[yy], fi_send.at[yy], fi_recv.at[yy], (me, yy * CORES + core)
+        )
+
+    def multiply(k):
+        j = order[k]
+        w_copies[k].wait()
+
+        @pl.loop(0, block_cols // TILE)
+        def _(n):
+            cols = pl.ds(pl.multiple_of(n * TILE, TILE), TILE)
+            term = row_term(qv[...], wv[j, cols, :]).astype(bf16)
+            for g in range(groups):
+                base = g * rows_dev
+                own_image[j, pl.ds(g * per_image, per_image), cols] = term[base : base + per_image]
+                own_text[j, g % CORES, g // CORES, :, cols] = term[base + per_image : base + rows_dev]
+
+        text_to_mate(k).start()
+
+    def add_image(yy):
+        image_to_mate(yy).wait_recv()
+
+        @pl.loop(0, image_rows // ROW_STEP)
+        def _(n):
+            rows = pl.ds(pl.multiple_of(n * ROW_STEP, ROW_STEP), ROW_STEP)
+            total = own_image[yy * CORES + core, rows].astype(f32) + mate_image[yy, rows].astype(f32)
+            sum_image[yy, rows] = total.astype(bf16)
+
+    def add_text(k):
+        j = order[k]
+        text_to_mate(k).wait_recv()
+        for yy in far:
+            @pl.loop(0, text_rows // ROW_STEP)
+            def _(n):
+                rows = pl.ds(pl.multiple_of(n * ROW_STEP, ROW_STEP), ROW_STEP)
+                total = own_text[j, core, yy, rows].astype(f32) + mate_text[j, yy, rows].astype(f32)
+                sum_text[j, yy, rows] = total.astype(bf16)
+
+    def send_text(k):
+        for yy in far:
+            text_to_far(k, yy).start()
+
+    q_copy.wait()
+    for k in range(early):
+        multiply(k)
+        if k % CORES == 0:
+            image_to_mate(far[k // CORES]).start() if k // CORES < len(far) else None
+    for yy in far[: early // CORES]:
+        add_image(yy)
+        image_to_far(yy).start()
+    weights.relay(1, 0)
+    for k in range(early):
+        add_text(k)
+        send_text(k)
+    for chunk in range(1, CHUNKS):
+        weights.relay(1, chunk)
+    for k in range(early, len(order)):
+        multiply(k)
+        if k % CORES == 0:
+            image_to_mate((far + [y])[k // CORES]).start()
+        if 2 < depth and k - early < CHUNKS:
+            weights.relay(2, k - early)
+    for yy in far[early // CORES :]:
+        add_image(yy)
+        image_to_far(yy).start()
+    for chunk in range(len(order) - early, CHUNKS):
+        weights.relay(2, chunk)
+
+    def use_weights(block):
+        cols = pl.ds(pl.multiple_of(block * shard_k, shard_k), shard_k)
+        x_acc[...] += jnp.dot(vision_ref[:, cols], w_all[block], preferred_element_type=f32)
+
+    own_cols = pl.ds(pl.multiple_of(me * shard_k, shard_k), shard_k)
+    x_acc[...] = jnp.dot(vision_ref[:, own_cols], proj_ref[...], preferred_element_type=f32)
+    weights.line_blocks(1, use_weights)
+    for hop in range(3, depth):
+        for chunk in range(CHUNKS):
+            weights.relay(hop, chunk)
+    for hop in range(2, depth):
+        weights.line_blocks(hop, use_weights)
+
+    def vision_to(step):
+        target = lax.rem(me + step, shards)
+        cols = pl.ds(pl.multiple_of(target * shard_k, shard_k), shard_k)
+        return remote(
+            vision_ref.at[:, cols], v_all.at[me], v_send.at[target], v_recv.at[me], (target, member)
+        )
+
+    def vision_from(step):
+        source = lax.rem(me + step, shards)
+        cols = pl.ds(pl.multiple_of(source * shard_k, shard_k), shard_k)
+        return remote(
+            vision_ref.at[:, cols], v_all.at[source], v_send.at[source], v_recv.at[source], (source, member)
+        )
+
+    for step in range(1, shards):
+        vision_to(step).start()
+
+    image_to_mate(y).wait_recv()
+    for yy in far:
+        image_from_far(yy).wait_recv()
+    member_cols = pl.ds(pl.multiple_of(member * block_cols, block_cols), block_cols)
+
+    @pl.loop(0, image_rows // ROW_STEP)
+    def _(n):
+        rows = pl.ds(pl.multiple_of(n * ROW_STEP, ROW_STEP), ROW_STEP)
+        total = own_image[member, rows].astype(f32) + mate_image[y, rows].astype(f32)
+        for yy in far:
+            total = total + far_image[yy, rows].astype(f32)
+        scaled_image[rows] = gain_ref[:, member_cols] * total
+
+    for k in range(early, len(order)):
+        add_text(k)
+    for hop in range(depth):
+        weights.side_blocks(hop, use_weights)
+
+    @pl.loop(0, image_rows // ROW_STEP)
+    def _(n):
+        rows = pl.ds(pl.multiple_of(n * ROW_STEP, ROW_STEP), ROW_STEP)
+        x = x_acc[rows].astype(bf16).astype(f32)
+        x_acc[rows] = x
+        squares = jnp.sum(x * x, axis=1, keepdims=True)
+        inner = jnp.sum(x * scaled_image[rows], axis=1, keepdims=True)
+        lane = lax.broadcasted_iota(jnp.int32, (ROW_STEP, 128), 1)
+        g_acc[rows, pl.ds(0, 128)] = jnp.where(lane == 0, squares, inner)
+
+    stat_own[...] = g_acc[:, 0:128].T[0:8]
+
+    def stat_to(step):
+        target = lax.rem(member + step, groups)
+        return remote(stat_own, stats.at[member], s_send.at[target], s_recv.at[member], (me, target))
+
+    def stat_from(step):
+        source = lax.rem(member + step, groups)
+        return remote(stat_own, stats.at[source], s_send.at[source], s_recv.at[source], (me, source))
+
+    for step in range(1, groups):
+        stat_to(step).start()
+    for k in range(early, len(order)):
+        send_text(k)
+    total = stat_own[...]
+    for step in range(1, groups):
+        stat_from(step).wait_recv()
+        total = total + stats[lax.rem(member + step, groups)]
+    spread = jnp.concatenate([total] * 16, axis=0).T
+    inv_all = lax.rsqrt(spread[:, 0:1] / width + norm_eps)
+    g_acc[:, 0:128] = jnp.broadcast_to(inv_all, (image_rows, 128))
+    g_acc[:, 128:256] = jnp.broadcast_to(inv_all**3 * (spread[:, 1:2] / width), (image_rows, 128))
+
+    @pl.loop(0, image_rows // ROW_STEP)
+    def _(n):
+        rows = pl.ds(pl.multiple_of(n * ROW_STEP, ROW_STEP), ROW_STEP)
+        inv, pull = g_acc[rows, pl.ds(0, 1)], g_acc[rows, pl.ds(128, 1)]
+        grad = inv * scaled_image[rows] - x_acc[rows] * pull
+        g_own[rows] = jnp.where(live_ref[rows] > 0, grad, 0.0).astype(bf16)
+
+    grads = LineGather(depth, me, member, g_own, g_all, c_send, c_recv)
+    grads.start()
+
+    def vision_term(left, right):
+        return lax.dot_general(left, right, (((0,), (0,)), ((), ())), preferred_element_type=f32)
+
+    def use_grads(block):
+        g_acc[...] += vision_term(v_all[block], g_all[block])
+
+    g_acc[...] = vision_term(vision_ref[:, own_cols], g_own[...])
+    for step in range(1, shards):
+        vision_from(step).wait_recv()
+    for hop in range(1, depth):
+        for chunk in range(CHUNKS):
+            grads.relay(hop, chunk)
+        if hop < depth - 1:
+            grads.line_blocks(hop, use_grads)
+    grads.line_blocks(depth - 1, use_grads)
+
+    for k in range(len(order)):
+        for yy in far:
+            text_from_far(k, yy).wait_recv()
+    t_copy.wait()
+
+    @pl.loop(0, text_rows // ROW_STEP)
+    def _(n):
+        rows = pl.ds(pl.multiple_of(n * ROW_STEP, ROW_STEP), ROW_STEP)
+        squares = jnp.zeros((ROW_STEP, 1), f32)
+        inner = jnp.zeros((ROW_STEP, 1), f32)
+        for j in range(groups):
+            cols = pl.ds(j * block_cols, block_cols)
+            x = tv[rows, cols].astype(f32)
+            norm = own_text[j, core, y, rows].astype(f32) + mate_text[j, y, rows].astype(f32)
+            for yy in far:
+                norm = norm + far_text[yy, j, rows].astype(f32)
+            scaled = gain_ref[:, cols] * norm
+            squares += jnp.sum(x * x, axis=1, keepdims=True)
+            inner += jnp.sum(x * scaled, axis=1, keepdims=True)
+        inv = lax.rsqrt(squares / width + norm_eps)
+        pull = inv**3 * (inner / width)
+        for j in range(groups):
+            cols = pl.ds(j * block_cols, block_cols)
+            x = tv[rows, cols].astype(f32)
+            norm = own_text[j, core, y, rows].astype(f32) + mate_text[j, y, rows].astype(f32)
+            for yy in far:
+                norm = norm + far_text[yy, j, rows].astype(f32)
+            text_out[rows, cols] = (inv * (gain_ref[:, cols] * norm) - x * pull).astype(bf16)
+
+    for hop in range(depth):
+        grads.side_blocks(hop, use_grads)
+    proj_out[...] = g_acc[...] * grad_scale
+
+    weights.drain()
+    grads.drain()
+    for step in range(1, shards):
+        vision_to(step).wait_send()
+    for step in range(1, groups):
+        stat_to(step).wait_send()
+    for k in range(len(order)):
+        text_to_mate(k).wait_send()
+        for yy in far:
+            text_to_far(k, yy).wait_send()
+    for yy in far + [y]:
+        image_to_mate(yy).wait_send()
+    for yy in far:
+        image_to_far(yy).wait_send()
+
+
+def live_rows(image_count, groups):
+    image_rows = IMG_MAX * PATCH
+    row_ids = jnp.arange(groups * image_rows, dtype=jnp.int32)
+    owners = row_ids // image_rows
+    slot_ids = row_ids % image_rows // PATCH
+    owner_match = owners[:, None] == jnp.arange(groups, dtype=jnp.int32)[None, :]
+    owner_counts = jnp.sum(jnp.where(owner_match, image_count[None, :], 0), axis=1)
+    return (slot_ids < owner_counts)[:, None]
+
+
+def fused_body(vision_rows, image_count, proj_flat, text_embeds, norm_gain, q_weight, q_grad):
+    groups, shards = lax.axis_size("mp"), lax.axis_size("dp")
+    model_width, bc = q_weight.shape
+    image_rows, enc_width = vision_rows.shape
+    text_rows = text_embeds.shape[0]
+    shard_k = proj_flat.shape[0] * proj_flat.shape[1] // bc
+    chips, depth = groups // CORES, shards // SIDE
+    live = live_rows(image_count, groups).astype(jnp.int32)
+    grad_scale = 1.0 / float(shards * image_rows) ** 0.5
+    f32, bf16 = jnp.float32, jnp.bfloat16
+    vmem, dma = pltpu.VMEM, pltpu.SemaphoreType.DMA
+    on_chip = pl.BlockSpec(memory_space=pltpu.VMEM)
+    anywhere = pl.BlockSpec(memory_space=pl.ANY)
+    text_grad, proj_block = pl.pallas_call(
+        functools.partial(kernel, shards, groups, grad_scale),
+        name="projector_backward",
+        out_shape=(
+            jax.ShapeDtypeStruct(text_embeds.shape, bf16),
+            jax.ShapeDtypeStruct((shard_k, bc), f32),
+        ),
+        in_specs=[on_chip] * 4 + [anywhere] * 3,
+        out_specs=(on_chip, on_chip),
+        scratch_shapes=[
+            vmem(q_grad.shape, bf16),
+            vmem((groups, bc, bc), bf16),
+            vmem(text_embeds.shape, bf16),
+            vmem((groups, CORES, chips, text_rows, bc), bf16),
+            vmem((groups, image_rows, bc), bf16),
+            vmem((groups, chips, text_rows, bc), bf16),
+            vmem((chips, image_rows, bc), bf16),
+            vmem((groups, chips, text_rows, bc), bf16),
+            vmem((chips, image_rows, bc), bf16),
+            vmem((chips, groups, text_rows, bc), bf16),
+            vmem((chips, image_rows, bc), bf16),
+            vmem((image_rows, bc), f32),
+            vmem((image_rows, bc), f32),
+            vmem((shard_k, bc), f32),
+            vmem((image_rows, bc), bf16),
+            vmem((8, image_rows), f32),
+            vmem((groups, 8, image_rows), f32),
+            vmem((shards, shard_k, bc), bf16),
+            vmem((shards, image_rows, bc), bf16),
+            vmem((shards, image_rows, shard_k), bf16),
+            dma, dma((groups,)), dma,
+            dma((3, depth, CHUNKS)), dma((shards, CHUNKS)),
+            dma((3, depth, CHUNKS)), dma((shards, CHUNKS)),
+            dma((shards,)), dma((shards,)),
+            dma((groups,)), dma((groups,)),
+            dma((chips,)), dma((chips,)),
+            dma((groups, chips)), dma((chips, groups)),
+            dma((chips,)), dma((chips,)),
+            dma((groups,)), dma((groups,)),
+        ],
+        compiler_params=pltpu.CompilerParams(
+            collective_id=0, has_side_effects=True, vmem_limit_bytes=56 * 1024 * 1024
+        ),
+    )(
+        proj_flat.reshape(shard_k, bc),
+        vision_rows,
+        live,
+        norm_gain[None, :],
+        q_grad,
+        q_weight.reshape(groups, bc, bc),
+        text_embeds,
+    )
+    return text_grad, proj_block.reshape(proj_flat.shape)
 
 
 def norm_back(rows_in, grads, gain):
@@ -25,7 +508,7 @@
     return inv_rms * scaled - inputs * inv_rms**3 * inner_mean
 
 
-def body(vision_rows, image_count, proj_flat, text_embeds, norm_gain, q_weight, q_grad):
+def general_body(vision_rows, image_count, proj_flat, text_embeds, norm_gain, q_weight, q_grad):
     groups = lax.axis_size("mp")
     member = lax.axis_index("mp")
     shards = lax.axis_size("dp")
@@ -39,12 +522,7 @@
     embed_cols = jnp.dot(vision_rows, proj_block, preferred_element_type=jnp.float32).astype(
         jnp.bfloat16
     )
-    row_ids = jnp.arange(groups * image_rows, dtype=jnp.int32)
-    owners = row_ids // image_rows
-    slot_ids = row_ids % image_rows // PATCH
-    owner_match = owners[:, None] == jnp.arange(groups, dtype=jnp.int32)[None, :]
-    owner_counts = jnp.sum(jnp.where(owner_match, image_count[None, :], 0), axis=1)
-    live_group = (slot_ids < owner_counts)[:, None]
+    live_group = live_rows(image_count, groups)
     blocks = q_grad.reshape(groups, ROWS_DEV, block_cols)
     image_query = blocks[:, :image_rows].reshape(-1, block_cols)
     text_query = blocks[:, image_rows:].reshape(-1, block_cols)
@@ -79,6 +557,26 @@
     return (text_grad, proj_grad)
 
 
+def body(vision_rows, image_count, proj_flat, text_embeds, norm_gain, q_weight, q_grad):
+    groups, shards = lax.axis_size("mp"), lax.axis_size("dp")
+    bc = q_weight.shape[1]
+    count = proj_flat.shape[0] * proj_flat.shape[1]
+    shard_k = count // bc
+    fits = (
+        count % bc == 0
+        and shard_k % 128 == 0
+        and shard_k * shards == vision_rows.shape[1]
+        and shard_k == vision_rows.shape[0]
+        and bc % TILE == 0
+        and groups > CORES
+        and groups % CORES == 0
+        and shards > SIDE
+        and shards % SIDE == 0
+    )
+    run = fused_body if fits else general_body
+    return run(vision_rows, image_count, proj_flat, text_embeds, norm_gain, q_weight, q_grad)
+
+
 def solution(mesh):
     return jax.shard_map(
         body,

time: 185 us -> 73.8 us (0.40)
  waiting for transfers between devices: 121 us -> 0 us
  Pallas kernels: 0 us -> 65.6 us
  matrix products: 22.1 us -> 0 us
  between operations: 15.8 us -> 0.65 us
  local copies, waits for them, and re-layouts: 16 us -> 5.89 us
  blocking collectives: 6.48 us -> 0 us
    reduce_scatter x3 -> x0, waiting for transfers between devices: 86.3 us -> none  [the longest x1 86.2 us: body(): proj_grad = lax.psum_scatter(padded, 'dp', scatter_dimension=0, tiled=True)]
    pallas_call x0 -> x1, Pallas kernels: none -> 65.6 us  [fused_body(): pl.pallas_call(functools.partial(kernel, shards, groups, grad_scale), nam...]
    all_gather x1 -> x0, waiting for transfers between devices: 34.4 us -> none  [body(): gathered = lax.all_gather(proj_flat, 'dp', axis=0, tiled=True)]
    dot_general x4 -> x0, matrix products: 22.1 us -> none  [the longest x2 17.7 us: row_term(): lax.dot_general(left, weight, (((1,), (1,)), ((), ())), preferred_element...]
    psum x1 -> x0, blocking collectives: 6.48 us -> none  [body(): lax.psum((jnp.sum(x_cols * x_cols, axis=1), jnp.sum(scaled * x_cols, axis...]
    mul x1 -> x0, local copies, waits for them, and re-layouts: 5.36 us -> none  [body(): lax.dot_general(vision_rows, image_cols, (((0,), (0,)), ((), ())), prefer...]
    another operation x1 -> x0, local copies, waits for them, and re-layouts: 3.01 us -> none  [body(): gathered.reshape(-1)[:used_count].reshape(enc_width, block_cols)]
    reshape x1 -> x2, local copies, waits for them, and re-layouts: 4.91 us -> 3.68 us  [the longest x1 1.92 us: fused_body(): return (text_grad, proj_block.reshape(proj_flat.shape))]
  transfers between devices with their start and end apart: 4 -> 0, of which waited for: 2 -> 0; matrix products, arithmetic and copies ran while one was open for 21% -> 0% of each run, Pallas kernels for 0% -> 0%
where the time goes in v1:
time: 73.8 us; the launch traced here: 73.6 us
  Pallas kernels  65.6 us (89%)
  local copies, waits for them, and re-layouts  5.89 us (8%)
  other arithmetic  1.4 us (2%)
    pallas_call x1, Pallas kernels, fused_body(): pl.pallas_call(functools.partial(kernel, shards, groups, grad_scale), nam...  65.6 us
    unnamed x1, local copies, waits for them, and re-layouts  2.06 us
    reshape x1, local copies, waits for them, and re-layouts, fused_body(): return (text_grad, proj_block.reshape(proj_flat.shape))  1.92 us
    reshape x1, local copies, waits for them, and re-layouts, fused_body(): proj_flat.reshape(shard_k, bc)  1.77 us

profile of v1, /device:TPU:0, one launch (start us, length us, event | category | flops | bytes accessed | tf_op | source)
XLA Modules:
  0.0 73.6 jit_solution(392995949319301752)
XLA Ops:
  0.6 0.7 %select_reduce_fusion = s32[128]{0:T(128)S(1)} fusion(s32[4]{0:T(128)} %param.8, s32[128]{0:T(128)S(1)} %and_select_fusion), kind=kLoop, calls=%fused_computation | loop fusion | flops 1408 | bytes 1040 | tf_op jit(solution)/shard_map/reduce_sum | solution.py:431
  1.4 0.1 copy.11
  1.5 0.6 convert_element_type.3.live_ref
  2.2 1.8 %reshape.105.proj_ref = bf16[128,1024]{1,0:T(8,128)(2,1)} reshape(bf16[1024,128]{1,0:T(8,128)(2,1)} %param.9) | data formatting | bytes 524288 | tf_op jit(solution)/shard_map/reshape | solution.py:492
  3.9 65.6 %projector_backward.1 = (bf16[96,4096]{1,0:T(8,128)(2,1)}, f32[128,1024]{1,0:T(8,128)}) custom-call(bf16[128,1024]{1,0:T(8,128)(2,1)} %reshape.105.proj_ref, bf16[128,1024]{1,0:T(8,128)(2,1)} %vision_ref.1, s32[128,1]{1,0:T(8,128)} %convert_element_type.3.live_ref, f32[1,4096]{1,0:T(1,128)} %bitcast.5, bf16[512,1024]{1,0:T(8,128)(2,1)} %q_hbm.1, ...), custom_call_target="tpu_custom_call" | custom-call | tf_op jit(solution)/shard_map/projector_backward/pallas_call | solution.py:448
  69.6 1.9 %reshape.107 = f32[1024,128]{1,0:T(8,128)} reshape(f32[128,1024]{1,0:T(8,128)} %get-tuple-element.5) | data formatting | bytes 1048576 | tf_op jit(solution)/shard_map/reshape | solution.py:500
  71.5 2.1 %copy.13 = bf16[96,4096]{1,0:T(8,128)(2,1)} copy(bf16[96,4096]{1,0:T(8,128)(2,1)} %get-tuple-element.8) | data formatting | bytes 1572864
  (2 shorter events, 0.0 us)

commit v2 on v1

--- a/solution.py
+++ b/solution.py
@@ -28,7 +28,8 @@
 
 
 class LineGather:
-    def __init__(self, depth, me, member, own, buf, send, recv):
+    def __init__(self, depth, me, member, own, buf, send, recv, turn):
+        self.turn_send = turn
         self.depth, self.me, self.member = depth, me, member
         self.z, self.x = me // SIDE, me % SIDE
         self.own, self.buf, self.send, self.recv = own, buf, send, recv
@@ -62,8 +63,34 @@
 
             self.copy(self.z, self.x, chunk, 2, True).start()
 
+    def turned(self, way):
+        block = (self.depth - 1 if way else 0) * SIDE + 1 - self.x
+        place = self.buf.at[block, self.rows(CHUNKS - 1)]
+        return pltpu.make_async_remote_copy(
+            src_ref=place,
+            dst_ref=place,
+            send_sem=self.turn_send.at[way],
+            recv_sem=self.recv.at[block, CHUNKS - 1],
+            device_id=(self.me - SIDE if way else self.me + SIDE, self.member),
+            device_id_type=MESH,
+        )
+
+    def turn(self, hop):
+        last = self.depth - 1
+        for way, place in ((0, self.z), (1, last - self.z)):
+            due = (place == hop) | (place == 0) if hop == 1 else place == hop
+
+            @pl.when(due)
+            def _():
+                self.turned(way).wait_recv()
+
+                @pl.when(place < last)
+                def _():
+                    self.turned(way).start()
+
     def relay(self, hop, chunk):
         below, above = self.z - hop, self.z + hop
+        final = chunk == CHUNKS - 1
 
         @pl.when(below >= 0)
         def _():
@@ -73,7 +100,9 @@
             def _():
                 self.copy(below, self.x, chunk, 0).start()
 
-            self.copy(below, self.x, chunk, 2).start()
+            @pl.when(below > 0 if final else below >= 0)
+            def _():
+                self.copy(below, self.x, chunk, 2).start()
 
         @pl.when(above < self.depth)
         def _():
@@ -83,7 +112,12 @@
             def _():
                 self.copy(above, self.x, chunk, 1).start()
 
-            self.copy(above, self.x, chunk, 2).start()
+            @pl.when(above < self.depth - 1 if final else above < self.depth)
+            def _():
+                self.copy(above, self.x, chunk, 2).start()
+
+        if final:
+            self.turn(hop)
 
     def line_blocks(self, hop, use):
         for zz in (self.z - hop, self.z + hop):
@@ -95,8 +129,13 @@
         for zz in (self.z,) if hop == 0 else (self.z - hop, self.z + hop):
             @pl.when((zz >= 0) & (zz < self.depth))
             def _():
-                for chunk in range(CHUNKS):
+                for chunk in range(CHUNKS - 1):
                     self.copy(zz, 1 - self.x, chunk, 2).wait_recv()
+
+                @pl.when((zz > 0) & (zz < self.depth - 1))
+                def _():
+                    self.copy(zz, 1 - self.x, CHUNKS - 1, 2).wait_recv()
+
                 use(zz * SIDE + 1 - self.x)
 
     def drain(self):
@@ -110,17 +149,26 @@
                 def _():
                     self.copy(zz, self.x, chunk, 1).wait_send()
 
-                self.copy(zz, self.x, chunk, 2).wait_send()
+                if chunk == CHUNKS - 1 and zz in (0, self.depth - 1):
+                    @pl.when(self.z == zz)
+                    def _():
+                        self.copy(zz, self.x, chunk, 2).wait_send()
+                else:
+                    self.copy(zz, self.x, chunk, 2).wait_send()
+        for way, place in ((0, self.z), (1, self.depth - 1 - self.z)):
+            @pl.when(place < self.depth - 1)
+            def _():
+                self.turned(way).wait_send()
 
 
 def kernel(
     shards, groups, grad_scale,
-    proj_ref, vision_ref, live_ref, gain_ref, q_hbm, w_hbm, text_hbm,
+    proj_ref, vision_ref, count_ref, gain_ref, q_hbm, w_hbm, text_hbm,
     text_out, proj_out,
     qv, wv, tv, own_text, own_image, mate_text, mate_image, sum_text, sum_image,
     far_text, far_image, scaled_image, x_acc, g_acc, g_own, stat_own, stats,
-    w_all, g_all, v_all,
-    q_sem, w_sem, t_sem, a_send, a_recv, c_send, c_recv, v_send, v_recv,
+    w_all, w_flat, g_all, v_all,
+    q_sem, w_sem, t_sem, a_send, a_recv, a_turn, c_send, c_recv, c_turn, v_send, v_recv, vm_send, vm_recv,
     mt_send, mt_recv, mi_send, mi_recv, ft_send, ft_recv, fi_send, fi_recv, s_send, s_recv,
 ):
     me, member = lax.axis_index("dp"), lax.axis_index("mp")
@@ -128,7 +176,8 @@
     chips = groups // CORES
     y, core = member // CORES, member % CORES
     mate = y * CORES + 1 - core
-    shard_k, block_cols = proj_ref.shape
+    shard_k, block_cols = proj_out.shape
+    fold = block_cols // 128
     image_rows = vision_ref.shape[0]
     per_image = image_rows // groups
     rows_dev = qv.shape[0] // groups
@@ -149,17 +198,31 @@
     t_copy.start()
 
     barrier = pltpu.get_barrier_semaphore()
-    for step in range(1, shards):
-        pl.semaphore_signal(
-            barrier, inc=1, device_id=(lax.rem(me + step, shards), member), device_id_type=MESH
-        )
+    z, x = me // SIDE, me % SIDE
+
+    @pl.when(z > 0)
+    def _():
+        pl.semaphore_signal(barrier, inc=1, device_id=(me - SIDE, member), device_id_type=MESH)
+
+    @pl.when(z < depth - 1)
+    def _():
+        pl.semaphore_signal(barrier, inc=1, device_id=(me + SIDE, member), device_id_type=MESH)
+
+    across = z * SIDE + 1 - x
+    pl.semaphore_signal(barrier, inc=1, device_id=(across, member), device_id_type=MESH)
     for step in range(1, groups):
         pl.semaphore_signal(
             barrier, inc=1, device_id=(me, lax.rem(member + step, groups)), device_id_type=MESH
         )
-    pl.semaphore_wait(barrier, shards + groups - 2)
-
-    weights = LineGather(depth, me, member, proj_ref, w_all, a_send, a_recv)
+    @pl.when((z > 0) & (z < depth - 1))
+    def _():
+        pl.semaphore_wait(barrier, 2 + groups)
+
+    @pl.when((z == 0) | (z == depth - 1))
+    def _():
+        pl.semaphore_wait(barrier, 1 + groups)
+
+    weights = LineGather(depth, me, member, proj_ref, w_all, a_send, a_recv, a_turn)
     weights.start()
 
     def remote(src, dst, send, recv, device):
@@ -266,12 +329,17 @@
     for chunk in range(len(order) - early, CHUNKS):
         weights.relay(2, chunk)
 
+    def wide(shard):
+        w_flat[...] = shard[...].astype(f32)
+        parts = [w_flat[pl.ds(c, shard_k, stride=fold), :] for c in range(fold)]
+        return jnp.concatenate(parts, axis=1).astype(bf16)
+
     def use_weights(block):
         cols = pl.ds(pl.multiple_of(block * shard_k, shard_k), shard_k)
-        x_acc[...] += jnp.dot(vision_ref[:, cols], w_all[block], preferred_element_type=f32)
+        x_acc[...] += jnp.dot(vision_ref[:, cols], wide(w_all.at[block]), preferred_element_type=f32)
 
     own_cols = pl.ds(pl.multiple_of(me * shard_k, shard_k), shard_k)
-    x_acc[...] = jnp.dot(vision_ref[:, own_cols], proj_ref[...], preferred_element_type=f32)
+    x_acc[...] = jnp.dot(vision_ref[:, own_cols], wide(proj_ref), preferred_element_type=f32)
     weights.line_blocks(1, use_weights)
     for hop in range(3, depth):
         for chunk in range(CHUNKS):
@@ -279,22 +347,33 @@
     for hop in range(2, depth):
         weights.line_blocks(hop, use_weights)
 
+    half = image_rows // CORES
+    my_half = pl.ds(pl.multiple_of(core * half, half), half)
+    mate_half = pl.ds(pl.multiple_of((1 - core) * half, half), half)
+
     def vision_to(step):
         target = lax.rem(me + step, shards)
         cols = pl.ds(pl.multiple_of(target * shard_k, shard_k), shard_k)
         return remote(
-            vision_ref.at[:, cols], v_all.at[me], v_send.at[target], v_recv.at[me], (target, member)
+            vision_ref.at[my_half, cols], v_all.at[me, my_half],
+            v_send.at[target], v_recv.at[me], (target, member),
         )
 
     def vision_from(step):
         source = lax.rem(me + step, shards)
         cols = pl.ds(pl.multiple_of(source * shard_k, shard_k), shard_k)
         return remote(
-            vision_ref.at[:, cols], v_all.at[source], v_send.at[source], v_recv.at[source], (source, member)
-        )
-
-    for step in range(1, shards):
-        vision_to(step).start()
+            vision_ref.at[my_half, cols], v_all.at[source, my_half],
+            v_send.at[source], v_recv.at[source], (source, member),
+        )
+
+    def vision_to_mate(source):
+        place = v_all.at[source, my_half]
+        return remote(place, place, vm_send.at[source], vm_recv.at[source], (me, mate))
+
+    def vision_from_mate(source):
+        place = v_all.at[source, mate_half]
+        return remote(place, place, vm_send.at[source], vm_recv.at[source], (me, mate))
 
     image_to_mate(y).wait_recv()
     for yy in far:
@@ -313,6 +392,8 @@
         add_text(k)
     for hop in range(depth):
         weights.side_blocks(hop, use_weights)
+    for step in range(1, shards):
+        vision_to(step).start()
 
     @pl.loop(0, image_rows // ROW_STEP)
     def _(n):
@@ -347,25 +428,32 @@
     g_acc[:, 0:128] = jnp.broadcast_to(inv_all, (image_rows, 128))
     g_acc[:, 128:256] = jnp.broadcast_to(inv_all**3 * (spread[:, 1:2] / width), (image_rows, 128))
 
-    @pl.loop(0, image_rows // ROW_STEP)
-    def _(n):
-        rows = pl.ds(pl.multiple_of(n * ROW_STEP, ROW_STEP), ROW_STEP)
-        inv, pull = g_acc[rows, pl.ds(0, 1)], g_acc[rows, pl.ds(128, 1)]
-        grad = inv * scaled_image[rows] - x_acc[rows] * pull
-        g_own[rows] = jnp.where(live_ref[rows] > 0, grad, 0.0).astype(bf16)
-
-    grads = LineGather(depth, me, member, g_own, g_all, c_send, c_recv)
+    for g in range(groups):
+        held = count_ref[g] * PATCH
+
+        @pl.loop(0, per_image // ROW_STEP)
+        def _(n):
+            first = n * ROW_STEP
+            rows = pl.ds(pl.multiple_of(g * per_image + first, ROW_STEP), ROW_STEP)
+            inv, pull = g_acc[rows, pl.ds(0, 1)], g_acc[rows, pl.ds(128, 1)]
+            grad = inv * scaled_image[rows] - x_acc[rows] * pull
+            slots = first + lax.broadcasted_iota(jnp.int32, (ROW_STEP, block_cols), 0)
+            g_own[rows] = jnp.where(slots < held, grad, 0.0).astype(bf16)
+
+    grads = LineGather(depth, me, member, g_own, g_all, c_send, c_recv, c_turn)
     grads.start()
 
     def vision_term(left, right):
         return lax.dot_general(left, right, (((0,), (0,)), ((), ())), preferred_element_type=f32)
 
     def use_grads(block):
+        vision_from_mate(block).wait_recv()
         g_acc[...] += vision_term(v_all[block], g_all[block])
 
     g_acc[...] = vision_term(vision_ref[:, own_cols], g_own[...])
     for step in range(1, shards):
         vision_from(step).wait_recv()
+        vision_to_mate(lax.rem(me + step, shards)).start()
     for hop in range(1, depth):
         for chunk in range(CHUNKS):
             grads.relay(hop, chunk)
@@ -410,6 +498,7 @@
     grads.drain()
     for step in range(1, shards):
         vision_to(step).wait_send()
+        vision_to_mate(lax.rem(me + step, shards)).wait_send()
     for step in range(1, groups):
         stat_to(step).wait_send()
     for k in range(len(order)):
@@ -439,11 +528,11 @@
     text_rows = text_embeds.shape[0]
     shard_k = proj_flat.shape[0] * proj_flat.shape[1] // bc
     chips, depth = groups // CORES, shards // SIDE
-    live = live_rows(image_count, groups).astype(jnp.int32)
     grad_scale = 1.0 / float(shards * image_rows) ** 0.5
     f32, bf16 = jnp.float32, jnp.bfloat16
     vmem, dma = pltpu.VMEM, pltpu.SemaphoreType.DMA
     on_chip = pl.BlockSpec(memory_space=pltpu.VMEM)
+    scalars = pl.BlockSpec(memory_space=pltpu.SMEM)
     anywhere = pl.BlockSpec(memory_space=pl.ANY)
     text_grad, proj_block = pl.pallas_call(
         functools.partial(kernel, shards, groups, grad_scale),
@@ -452,7 +541,7 @@
             jax.ShapeDtypeStruct(text_embeds.shape, bf16),
             jax.ShapeDtypeStruct((shard_k, bc), f32),
         ),
-        in_specs=[on_chip] * 4 + [anywhere] * 3,
+        in_specs=[on_chip, on_chip, scalars, on_chip] + [anywhere] * 3,
         out_specs=(on_chip, on_chip),
         scratch_shapes=[
             vmem(q_grad.shape, bf16),
@@ -472,13 +561,14 @@
             vmem((image_rows, bc), bf16),
             vmem((8, image_rows), f32),
             vmem((groups, 8, image_rows), f32),
-            vmem((shards, shard_k, bc), bf16),
+            vmem((shards,) + proj_flat.shape, bf16),
+            vmem(proj_flat.shape, f32),
             vmem((shards, image_rows, bc), bf16),
             vmem((shards, image_rows, shard_k), bf16),
             dma, dma((groups,)), dma,
-            dma((3, depth, CHUNKS)), dma((shards, CHUNKS)),
-            dma((3, depth, CHUNKS)), dma((shards, CHUNKS)),
-            dma((shards,)), dma((shards,)),
+            dma((3, depth, CHUNKS)), dma((shards, CHUNKS)), dma((2,)),
+            dma((3, depth, CHUNKS)), dma((shards, CHUNKS)), dma((2,)),
+            dma((shards,)), dma((shards,)), dma((shards,)), dma((shards,)),
             dma((groups,)), dma((groups,)),
             dma((chips,)), dma((chips,)),
             dma((groups, chips)), dma((chips, groups)),
@@ -489,9 +579,9 @@
             collective_id=0, has_side_effects=True, vmem_limit_bytes=56 * 1024 * 1024
         ),
     )(
-        proj_flat.reshape(shard_k, bc),
+        proj_flat,
         vision_rows,
-        live,
+        image_count,
         norm_gain[None, :],
         q_grad,
         q_weight.reshape(groups, bc, bc),
@@ -570,6 +660,8 @@
         and bc % TILE == 0
         and groups > CORES
         and groups % CORES == 0
+        and vision_rows.shape[0] // groups % ROW_STEP == 0
+        and text_embeds.shape[0] % ROW_STEP == 0
         and shards > SIDE
         and shards % SIDE == 0
     )

time: 73.8 us -> 67.1 us (0.909)
  Pallas kernels: 65.6 us -> 62.2 us
  local copies, waits for them, and re-layouts: 5.89 us -> 3.98 us
  other arithmetic: 1.4 us -> 0 us
    pallas_call x1, Pallas kernels: 65.6 us -> 62.2 us  [fused_body(): pl.pallas_call(functools.partial(kernel, shards, groups, grad_scale), nam...]
    reshape x1 -> x0, local copies, waits for them, and re-layouts: 1.77 us -> none  [fused_body(): proj_flat.reshape(shard_k, bc)]
    reduce_sum x1 -> x0, other arithmetic: 0.74 us -> none  [live_rows(): jnp.sum(jnp.where(owner_match, image_count[None, :], 0), axis=1)]
where the time goes in v2:
time: 67.1 us; the launch traced here: 66.8 us
  Pallas kernels  62.2 us (93%)
  local copies, waits for them, and re-layouts  3.98 us (6%)
    pallas_call x1, Pallas kernels, fused_body(): pl.pallas_call(functools.partial(kernel, shards, groups, grad_scale), nam...  62.2 us
    unnamed x1, local copies, waits for them, and re-layouts  2.06 us
    reshape x1, local copies, waits for them, and re-layouts, fused_body(): return (text_grad, proj_block.reshape(proj_flat.shape))  1.92 us

profile of v2, /device:TPU:0, one launch (start us, length us, event | category | flops | bytes accessed | tf_op | source)
XLA Modules:
  0.0 66.8 jit_solution(17304246605801627457)
XLA Ops:
  0.6 62.2 %projector_backward.1 = (bf16[96,4096]{1,0:T(8,128)(2,1)}, f32[128,1024]{1,0:T(8,128)}) custom-call(bf16[1024,128]{1,0:T(8,128)(2,1)} %proj_ref.1, bf16[128,1024]{1,0:T(8,128)(2,1)} %vision_ref.1, s32[4]{0:T(128)} %count_ref.1, f32[1,4096]{1,0:T(1,128)} %bitcast.3, bf16[512,1024]{1,0:T(8,128)(2,1)} %q_hbm.1, bf16[4,1024,1024]{2,1,0:T(8,128)(2,1)} %bitcast.2, ...), custom_call_target="tpu_custom_call" | custom-call | tf_op jit(solution)/shard_map/projector_backward/pallas_call | solution.py:537
  62.8 1.9 %reshape.11 = f32[1024,128]{1,0:T(8,128)} reshape(f32[128,1024]{1,0:T(8,128)} %get-tuple-element.5) | data formatting | bytes 1048576 | tf_op jit(solution)/shard_map/reshape | solution.py:590
  64.8 2.1 %copy.10 = bf16[96,4096]{1,0:T(8,128)(2,1)} copy(bf16[96,4096]{1,0:T(8,128)(2,1)} %get-tuple-element.8) | data formatting | bytes 1572864

commit v3 on v2

--- a/solution.py
+++ b/solution.py
@@ -12,7 +12,9 @@
 ROWS_DEV = 128
 CORES = 2
 SIDE = 2
-CHUNKS = 2
+CHUNKS = 4
+TURNED = 1
+PIECES = 2
 TILE = 256
 ROW_STEP = 16
 
@@ -63,14 +65,14 @@
 
             self.copy(self.z, self.x, chunk, 2, True).start()
 
-    def turned(self, way):
+    def turned(self, way, chunk):
         block = (self.depth - 1 if way else 0) * SIDE + 1 - self.x
-        place = self.buf.at[block, self.rows(CHUNKS - 1)]
+        place = self.buf.at[block, self.rows(chunk)]
         return pltpu.make_async_remote_copy(
             src_ref=place,
             dst_ref=place,
-            send_sem=self.turn_send.at[way],
-            recv_sem=self.recv.at[block, CHUNKS - 1],
+            send_sem=self.turn_send.at[way, chunk],
+            recv_sem=self.recv.at[block, chunk],
             device_id=(self.me - SIDE if way else self.me + SIDE, self.member),
             device_id_type=MESH,
         )
@@ -82,15 +84,16 @@
 
             @pl.when(due)
             def _():
-                self.turned(way).wait_recv()
-
-                @pl.when(place < last)
-                def _():
-                    self.turned(way).start()
+                for chunk in range(CHUNKS - TURNED, CHUNKS):
+                    self.turned(way, chunk).wait_recv()
+
+                    @pl.when(place < last)
+                    def _():
+                        self.turned(way, chunk).start()
 
     def relay(self, hop, chunk):
         below, above = self.z - hop, self.z + hop
-        final = chunk == CHUNKS - 1
+        final = chunk >= CHUNKS - TURNED
 
         @pl.when(below >= 0)
         def _():
@@ -116,7 +119,7 @@
             def _():
                 self.copy(above, self.x, chunk, 2).start()
 
-        if final:
+        if chunk == CHUNKS - 1:
             self.turn(hop)
 
     def line_blocks(self, hop, use):
@@ -129,12 +132,13 @@
         for zz in (self.z,) if hop == 0 else (self.z - hop, self.z + hop):
             @pl.when((zz >= 0) & (zz < self.depth))
             def _():
-                for chunk in range(CHUNKS - 1):
+                for chunk in range(CHUNKS - TURNED):
                     self.copy(zz, 1 - self.x, chunk, 2).wait_recv()
 
                 @pl.when((zz > 0) & (zz < self.depth - 1))
                 def _():
-                    self.copy(zz, 1 - self.x, CHUNKS - 1, 2).wait_recv()
+                    for chunk in range(CHUNKS - TURNED, CHUNKS):
+                        self.copy(zz, 1 - self.x, chunk, 2).wait_recv()
 
                 use(zz * SIDE + 1 - self.x)
 
@@ -149,7 +153,7 @@
                 def _():
                     self.copy(zz, self.x, chunk, 1).wait_send()
 
-                if chunk == CHUNKS - 1 and zz in (0, self.depth - 1):
+                if chunk >= CHUNKS - TURNED and zz in (0, self.depth - 1):
                     @pl.when(self.z == zz)
                     def _():
                         self.copy(zz, self.x, chunk, 2).wait_send()
@@ -158,7 +162,8 @@
         for way, place in ((0, self.z), (1, self.depth - 1 - self.z)):
             @pl.when(place < self.depth - 1)
             def _():
-                self.turned(way).wait_send()
+                for chunk in range(CHUNKS - TURNED, CHUNKS):
+                    self.turned(way, chunk).wait_send()
 
 
 def kernel(
@@ -176,7 +181,7 @@
     chips = groups // CORES
     y, core = member // CORES, member % CORES
     mate = y * CORES + 1 - core
-    shard_k, block_cols = proj_out.shape
+    shard_k, block_cols = g_acc.shape
     fold = block_cols // 128
     image_rows = vision_ref.shape[0]
     per_image = image_rows // groups
@@ -492,7 +497,8 @@
 
     for hop in range(depth):
         grads.side_blocks(hop, use_grads)
-    proj_out[...] = g_acc[...] * grad_scale
+    for c in range(fold):
+        proj_out[pl.ds(c, shard_k, stride=fold), :] = g_acc[:, c * 128 : (c + 1) * 128] * grad_scale
 
     weights.drain()
     grads.drain()
@@ -509,6 +515,27 @@
         image_to_mate(yy).wait_send()
     for yy in far:
         image_to_far(yy).wait_send()
+
+
+def place_outputs(text_in, proj_in, text_out, proj_out, text_held, proj_held, in_sem, out_sem):
+    def copies(refs, sem):
+        found = []
+        for k, (src, dst) in enumerate(refs):
+            step = src.shape[0] // PIECES
+            for p in range(PIECES):
+                rows = pl.ds(p * step, step)
+                found.append(pltpu.make_async_copy(src.at[rows], dst.at[rows], sem.at[k, p]))
+        return found
+
+    into = copies(((text_in, text_held), (proj_in, proj_held)), in_sem)
+    back = copies(((text_held, text_out), (proj_held, proj_out)), out_sem)
+    for copy in into:
+        copy.start()
+    for first, second in zip(into, back):
+        first.wait()
+        second.start()
+    for copy in back:
+        copy.wait()
 
 
 def live_rows(image_count, groups):
@@ -539,7 +566,7 @@
         name="projector_backward",
         out_shape=(
             jax.ShapeDtypeStruct(text_embeds.shape, bf16),
-            jax.ShapeDtypeStruct((shard_k, bc), f32),
+            jax.ShapeDtypeStruct(proj_flat.shape, f32),
         ),
         in_specs=[on_chip, on_chip, scalars, on_chip] + [anywhere] * 3,
         out_specs=(on_chip, on_chip),
@@ -566,8 +593,8 @@
             vmem((shards, image_rows, bc), bf16),
             vmem((shards, image_rows, shard_k), bf16),
             dma, dma((groups,)), dma,
-            dma((3, depth, CHUNKS)), dma((shards, CHUNKS)), dma((2,)),
-            dma((3, depth, CHUNKS)), dma((shards, CHUNKS)), dma((2,)),
+            dma((3, depth, CHUNKS)), dma((shards, CHUNKS)), dma((2, CHUNKS)),
+            dma((3, depth, CHUNKS)), dma((shards, CHUNKS)), dma((2, CHUNKS)),
             dma((shards,)), dma((shards,)), dma((shards,)), dma((shards,)),
             dma((groups,)), dma((groups,)),
             dma((chips,)), dma((chips,)),
@@ -587,7 +614,15 @@
         q_weight.reshape(groups, bc, bc),
         text_embeds,
     )
-    return text_grad, proj_block.reshape(proj_flat.shape)
+    kinds = (text_grad, proj_block)
+    return pl.pallas_call(
+        place_outputs,
+        name="place_outputs",
+        out_shape=tuple(jax.ShapeDtypeStruct(a.shape, a.dtype) for a in kinds),
+        in_specs=[anywhere] * 2,
+        out_specs=(anywhere, anywhere),
+        scratch_shapes=[vmem(a.shape, a.dtype) for a in kinds] + [dma((2, PIECES)), dma((2, PIECES))],
+    )(*kinds)
 
 
 def norm_back(rows_in, grads, gain):
@@ -661,7 +696,7 @@
         and groups > CORES
         and groups % CORES == 0
         and vision_rows.shape[0] // groups % ROW_STEP == 0
-        and text_embeds.shape[0] % ROW_STEP == 0
+        and text_embeds.shape[0] % (PIECES * ROW_STEP) == 0
         and shards > SIDE
         and shards % SIDE == 0
     )

time: 67.1 us -> 62.9 us (0.937)
  local copies, waits for them, and re-layouts: 3.98 us -> 0 us
    pallas_call x1, Pallas kernels: 62.2 us -> 60 us  [fused_body(): pl.pallas_call(functools.partial(kernel, shards, groups, grad_scale), nam...]
    pallas_call x0 -> x1, Pallas kernels: none -> 2.11 us  [fused_body(): pl.pallas_call(place_outputs, name='place_outputs', out_shape=tuple((jax....]
    unnamed x1 -> x0, local copies, waits for them, and re-layouts: 2.06 us -> none
    reshape x1 -> x0, local copies, waits for them, and re-layouts: 1.92 us -> none  [fused_body(): return (text_grad, proj_block.reshape(proj_flat.shape))]
where the time goes in v3:
time: 62.9 us; the launch traced here: 62.7 us
  Pallas kernels  62.1 us (99%)
  between operations  0.64 us (1%)
    pallas_call x1, Pallas kernels, fused_body(): pl.pallas_call(functools.partial(kernel, shards, groups, grad_scale), nam...  60 us
    pallas_call x1, Pallas kernels, fused_body(): pl.pallas_call(place_outputs, name='place_outputs', out_shape=tuple((jax....  2.11 us

profile of v3, /device:TPU:0, one launch (start us, length us, event | category | flops | bytes accessed | tf_op | source)
XLA Modules:
  0.0 62.7 jit_solution(3424985974982901757)
XLA Ops:
  0.6 60.0 %projector_backward.1 = (bf16[96,4096]{1,0:T(8,128)(2,1)}, f32[1024,128]{1,0:T(8,128)}) custom-call(bf16[1024,128]{1,0:T(8,128)(2,1)} %proj_ref.1, bf16[128,1024]{1,0:T(8,128)(2,1)} %vision_ref.1, s32[4]{0:T(128)} %count_ref.1, f32[1,4096]{1,0:T(1,128)} %bitcast.3, bf16[512,1024]{1,0:T(8,128)(2,1)} %q_hbm.1, bf16[4,1024,1024]{2,1,0:T(8,128)(2,1)} %bitcast.2, ...), custom_call_target="tpu_custom_call" | custom-call | tf_op jit(solution)/shard_map/projector_backward/pallas_call | solution.py:564
  60.6 2.1 %place_outputs.1 = (bf16[96,4096]{1,0:T(8,128)(2,1)}, f32[1024,128]{1,0:T(8,128)}) custom-call(bf16[96,4096]{1,0:T(8,128)(2,1)} %get-tuple-element.4.text_in, f32[1024,128]{1,0:T(8,128)} %get-tuple-element.5.proj_in), custom_call_target="tpu_custom_call" | custom-call | tf_op jit(solution)/shard_map/place_outputs/pallas_call | solution.py:618
